TPU v7x, 32 devices: a whole 2x2x4 slice. The times are simulated.
32 devices in a mesh: tile: 8 (over z, x), sub: 4 (over y, core).
Axes of the slice: x: 2, y: 2, z: 4, core: 2. Of those that a mesh axis runs over, the one named last changes fastest.
Arguments:
- grid_feats: bfloat16 [4096, 512], P(('tile', 'sub')), may hold values from -6 to 6
- mesh_feats: bfloat16 [4096, 512], P(('tile', 'sub')), may hold values from -6 to 6
- encode_edges: bfloat16 [32768, 512], P(('tile', 'sub')), may hold values from -6 to 6
- decode_edges: bfloat16 [16384, 512], P(('tile', 'sub')), may hold values from -6 to 6
- encode_source: int32 [32768], P(('tile', 'sub')), may hold values from 0 to 4095, as said below
- encode_target: int32 [32768], P(('tile', 'sub')), may hold values from -1 to 4095, as said below
- decode_source: int32 [16384], P(('tile', 'sub')), may hold values from 0 to 4095, as said below
- decode_target: int32 [16384], P(('tile', 'sub')), may hold values from -1 to 4095, as said below
- owner_fine: int32 [4096], P(('tile', 'sub')), may hold values from 0 to 1023, as said below
- owner_coarse: int32 [1024], P('tile'), may hold values from 0 to 511
- encode_weight: bfloat16 [512, 512], replicated, may hold values from -0.25 to 0.25
- decode_weight: bfloat16 [512, 512], replicated, may hold values from -0.25 to 0.25
- middle_weight: bfloat16 [512, 512], replicated, may hold values from -0.25 to 0.25
- summit_weight: bfloat16 [512, 512], replicated, may hold values from -0.25 to 0.25
- cotangent: bfloat16 [4096, 512], P(('tile', 'sub')), may hold values from -6 to 6
Outputs:
- grid_update: bfloat16 [4096, 512], P(('tile', 'sub'))
- encode_grad: float32 [512, 512], replicated
- decode_grad: float32 [512, 512], replicated
- middle_grad: float32 [512, 512], replicated
- summit_grad: float32 [512, 512], replicated
Inputs may be any that keep to these rules, and one draw needn't show every extreme that they name: `encode_source`: edge slot e is listed on device d = e // 1024; its source grid node lies on device d - 1, d or d + 1. `encode_target`: -1 marks padding; every other value is a mesh node of the device that lists the slot. On each device padding fills whole blocks of 128 slots after all live ones; every device has a live block, and some device has no padding. `decode_source`: edge slot e is listed on device d = e // 512; its source mesh node lies on device d - 1, d or d + 1. `decode_target`: -1 marks padding; every other value is a grid node of the device that lists the slot. On each device padding fills whole blocks of 128 slots after all live ones; every device has a live block, and some device has no padding. `owner_fine`: the middle node of fine mesh node m lies on the tile of the device that holds m.
All inputs are finite; a program needn't handle non-finite values.
Results may differ from a plain program's by a relative error of at most 0.012.
Values may be sent and summed in bfloat16 or wider, within the bound.
No kernel may reach another device: no remote copies, remote signals or barrier semaphores. Data moves between devices by JAX's collectives and lax.ppermute only.
A program may use at most 64 MiB of HBM per device.

v0:
```python
import jax
import jax.numpy as jnp
from jax import lax
from jax.sharding import PartitionSpec as P

TOP_NODES = 512
BLOCK = 128


def extended(x, sides, width):
    for axis, dim in sides:
        peers, length = (lax.axis_size(axis), x.shape[dim])
        up = [(i, (i + 1) % peers) for i in range(peers - 1)]
        down = [(j, i) for i, j in up]
        last = lax.slice_in_dim(x, length - width, length, axis=dim)
        initial = lax.slice_in_dim(x, 0, width, axis=dim)
        before = lax.ppermute(last, axis, up)
        after = lax.ppermute(initial, axis, down)
        x = jnp.concatenate([before, x, after], axis=dim)
    return x


def from_behind(x, axis, by):
    peers = lax.axis_size(axis)
    pairs = [(i, i + by) for i in range(peers) if 0 <= i + by < peers]
    return lax.ppermute(x, axis, pairs)


def silu_slope(values):
    sigmoid = jax.nn.sigmoid(values)
    return sigmoid * (1.0 + values * (1.0 - sigmoid))


def live_count(targets):
    heads = targets.reshape(-1, BLOCK)[:, 0]
    return jnp.sum((heads >= 0).astype(jnp.int32))


def local_targets(targets, first, limit):
    return jnp.where(targets >= 0, targets - first, limit)


def outer_sum(left, right):
    return lax.dot_general(
        left, right, (((0,), (0,)), ((), ())), preferred_element_type=jnp.float32
    )


def times_transposed(left, right):
    return lax.dot_general(
        left, right, (((1,), (1,)), ((), ())), preferred_element_type=jnp.float32
    )


def membership(indices, rows, dtype):
    return (jnp.arange(rows, dtype=jnp.int32)[:, None] == indices[None, :]).astype(dtype)


def exact_sum(members, values):
    return jnp.dot(
        members, values, precision=lax.Precision.HIGHEST, preferred_element_type=jnp.float32
    )


def edge_forward(sources, senders, targets, edge_feats, weight, segments, blocks):
    features = weight.shape[1]

    def block_step(block_id, carried):
        summed, stored = carried
        offset = block_id * BLOCK
        picked = lax.dynamic_slice_in_dim(senders, offset, BLOCK)
        receivers = lax.dynamic_slice_in_dim(targets, offset, BLOCK)
        edge_part = lax.dynamic_slice_in_dim(edge_feats, offset, BLOCK, 0)
        fetched = jnp.take(sources, picked, axis=0)
        preact = jnp.dot(fetched, weight, preferred_element_type=jnp.float32) + edge_part.astype(
            jnp.float32
        )
        summed = summed + exact_sum(
            membership(receivers, segments, jnp.float32), jax.nn.silu(preact)
        )
        stored = lax.dynamic_update_slice_in_dim(stored, preact, offset, 0)
        return (summed, stored)

    start_sum = jnp.zeros((segments, features), jnp.float32)
    start_store = jnp.zeros((senders.shape[0], features), jnp.float32)
    return lax.fori_loop(0, blocks, block_step, (start_sum, start_store))


def edge_backward(
    sources, senders, targets, stored, weight, upstream, factor, blocks, returned_rows
):
    features = weight.shape[1]

    def block_step(block_id, carried):
        gradient, returned = carried
        offset = block_id * BLOCK
        picked = lax.dynamic_slice_in_dim(senders, offset, BLOCK)
        receivers = lax.dynamic_slice_in_dim(targets, offset, BLOCK)
        preact = lax.dynamic_slice_in_dim(stored, offset, BLOCK, 0)
        fetched = jnp.take(sources, picked, axis=0)
        incoming = jnp.take(upstream, receivers, axis=0).astype(jnp.float32) * factor
        slope = (incoming * silu_slope(preact)).astype(jnp.bfloat16)
        gradient = gradient + outer_sum(fetched, slope)
        if returned_rows:
            passed = times_transposed(slope, weight)
            returned = returned + exact_sum(membership(picked, returned_rows, jnp.float32), passed)
        return (gradient, returned)

    start_grad = jnp.zeros((features, features), jnp.float32)
    start_back = jnp.zeros((max(returned_rows, 1), features), jnp.float32)
    return lax.fori_loop(0, blocks, block_step, (start_grad, start_back))


def shards(
    grid_feats,
    mesh_feats,
    encode_edges,
    decode_edges,
    encode_source,
    encode_target,
    decode_source,
    decode_target,
    owner_fine,
    owner_coarse,
    encode_weight,
    decode_weight,
    middle_weight,
    summit_weight,
    cotangent,
):
    grid_rows = grid_feats.shape[0]
    mesh_rows = mesh_feats.shape[0]
    level_rows = owner_coarse.shape[0]
    tiles = lax.axis_size("tile")
    subs = lax.axis_size("sub")
    device = lax.axis_index(("tile", "sub"))
    tile_id = lax.axis_index("tile")
    encode_factor = mesh_rows / encode_source.shape[0]
    decode_factor = grid_rows / decode_source.shape[0]
    middle_factor = level_rows / (mesh_rows * subs)
    summit_factor = TOP_NODES / (level_rows * tiles)
    grid_wide = extended(grid_feats, ((("tile", "sub"), 0),), grid_rows)
    encode_senders = encode_source - (device - 1) * grid_rows
    encode_targets = local_targets(encode_target, device * mesh_rows, mesh_rows)
    encode_blocks = live_count(encode_target)
    encode_summed, encode_stored = edge_forward(
        grid_wide,
        encode_senders,
        encode_targets,
        encode_edges,
        encode_weight,
        mesh_rows,
        encode_blocks,
    )
    mesh_mid = (mesh_feats.astype(jnp.float32) + encode_factor * encode_summed).astype(jnp.bfloat16)
    fine_local = owner_fine - tile_id * level_rows
    fine_members = membership(fine_local, level_rows, jnp.bfloat16)
    middle_part = jnp.dot(fine_members, mesh_mid, preferred_element_type=jnp.float32)
    middle_sum = lax.psum(middle_part, "sub")
    middle_in = (middle_factor * middle_sum).astype(jnp.bfloat16)
    middle_act = jnp.dot(middle_in, middle_weight, preferred_element_type=jnp.float32)
    middle_out = (middle_in.astype(jnp.float32) + jax.nn.silu(middle_act)).astype(jnp.bfloat16)
    top_members = membership(owner_coarse, TOP_NODES, jnp.bfloat16)
    summit_part = jnp.dot(top_members, middle_out, preferred_element_type=jnp.float32)
    summit_whole = lax.psum(summit_part, "tile")
    summit_in = (summit_factor * summit_whole).astype(jnp.bfloat16)
    summit_act = jnp.dot(summit_in, summit_weight, preferred_element_type=jnp.float32)
    summit_out = jax.nn.silu(summit_act).astype(jnp.bfloat16)
    coarse_of = jnp.take(owner_coarse, fine_local)
    lifted = jnp.take(middle_out, fine_local, axis=0).astype(jnp.float32) + jnp.take(
        summit_out, coarse_of, axis=0
    ).astype(jnp.float32)
    mesh_out = (mesh_mid.astype(jnp.float32) + lifted).astype(jnp.bfloat16)
    mesh_wide = extended(mesh_out, ((("tile", "sub"), 0),), mesh_rows)
    decode_senders = decode_source - (device - 1) * mesh_rows
    decode_targets = local_targets(decode_target, device * grid_rows, grid_rows)
    decode_blocks = live_count(decode_target)
    decode_summed, decode_stored = edge_forward(
        mesh_wide,
        decode_senders,
        decode_targets,
        decode_edges,
        decode_weight,
        grid_rows,
        decode_blocks,
    )
    grid_update = (grid_feats.astype(jnp.float32) + decode_factor * decode_summed).astype(
        jnp.bfloat16
    )
    decode_local, decode_returned = edge_backward(
        mesh_wide,
        decode_senders,
        decode_targets,
        decode_stored,
        decode_weight,
        cotangent,
        decode_factor,
        decode_blocks,
        3 * mesh_rows,
    )
    from_next = from_behind(decode_returned[:mesh_rows], ("tile", "sub"), -1)
    from_prev = from_behind(decode_returned[2 * mesh_rows :], ("tile", "sub"), 1)
    mesh_grad = decode_returned[mesh_rows : 2 * mesh_rows] + from_next + from_prev
    level_part = exact_sum(fine_members.astype(jnp.float32), mesh_grad)
    level_grad = lax.psum(level_part, "sub")
    summit_grad_part = exact_sum(top_members.astype(jnp.float32), level_grad)
    summit_grad_whole = lax.psum(summit_grad_part, "tile")
    summit_slope = (summit_grad_whole * silu_slope(summit_act)).astype(jnp.bfloat16)
    summit_local = outer_sum(summit_in, summit_slope)
    summit_back = times_transposed(summit_slope, summit_weight).astype(jnp.bfloat16)
    level_total = level_grad + summit_factor * jnp.take(summit_back, owner_coarse, axis=0).astype(
        jnp.float32
    )
    middle_slope = (level_total * silu_slope(middle_act)).astype(jnp.bfloat16)
    middle_local = outer_sum(middle_in, middle_slope)
    middle_back = level_total + times_transposed(middle_slope, middle_weight)
    mesh_total = mesh_grad + middle_factor * jnp.take(middle_back, fine_local, axis=0)
    encode_local, unused_rows = edge_backward(
        grid_wide,
        encode_senders,
        encode_targets,
        encode_stored,
        encode_weight,
        mesh_total,
        encode_factor,
        encode_blocks,
        0,
    )
    sub_share = 1.0 / subs
    encode_grad, decode_grad, middle_grad = lax.psum(
        (encode_local, decode_local, sub_share * middle_local), ("tile", "sub")
    )
    return (grid_update, encode_grad, decode_grad, middle_grad, summit_local)


def solution(mesh):
    placed = (
        P(("tile", "sub"), None),
        P(("tile", "sub"), None),
        P(("tile", "sub"), None),
        P(("tile", "sub"), None),
        P(("tile", "sub")),
        P(("tile", "sub")),
        P(("tile", "sub")),
        P(("tile", "sub")),
        P(("tile", "sub")),
        P("tile"),
        P(),
        P(),
        P(),
        P(),
        P(("tile", "sub"), None),
    )
    return jax.shard_map(
        shards,
        mesh=mesh,
        in_specs=placed,
        out_specs=(P(("tile", "sub"), None), P(), P(), P(), P()),
        check_vma=False,
    )
```

profile of v0, /device:TPU:0, one launch (start us, length us, event | category | flops | bytes accessed | tf_op | source)
XLA Modules:
  0.0 564.3 jit_solution(5614955575473783883)
XLA Ops:
  7.2 2.5 collective-permute-start
  15.4 1.6 broadcast_in_dim.93
  17.0 16.3 %while.46 = (s32[]{:T(128)}, f32[128,512]{1,0:T(8,128)S(1)}, f32[1024,512]{1,0:T(8,128)}, s32[]{:T(128)}, s32[1024]{0:T(1024)S(1)}, /*index=5*/s32[1024]{0:T(102...) while((s32[]{:T(128)}, f32[128,512]{1,0:T(8,128)S(1)}, ...), condition=%wide.region_3.5_spmd, body=%wide.region_2.0_spmd.sunk | while | flops 168314624 | bytes 2367415 | solution.py:86
  18.6 1.9 constant_dynamic-update-slice_fusion.7
  22.5 1.9 constant_dynamic-update-slice_fusion.7
  26.5 1.9 constant_dynamic-update-slice_fusion.7
  30.4 1.9 constant_dynamic-update-slice_fusion.7
  34.4 52.0 %all-reduce.7.cloned.1.call-done = f32[128,512]{1,0:T(8,128)} async-done(((f32[128,512]{1,0:T(8,128)}), f32[128,512]{1,0:T(8,128)}) %all-reduce.7.cloned.1.call-update) | async-done | bytes 262160 | tf_op jit(solution)/shard_map/psum | solution.py:159
  86.4 2.0 add_convert_fusion.2
  91.9 76.8 %all-reduce.9.cloned.1.call-done = f32[512,512]{1,0:T(8,128)} async-done(((f32[512,512]{1,0:T(8,128)}), f32[512,512]{1,0:T(8,128)}) %all-reduce.9.cloned.1.call-update) | async-done | bytes 1048592 | tf_op jit(solution)/shard_map/psum | solution.py:165
  168.7 2.7 multiply_convert_fusion.6
  172.4 1.7 collective-permute-start.2
  176.7 2.0 collective-permute-done.3
  179.6 19.5 %while.47 = (s32[]{:T(128)}, f32[128,512]{1,0:T(8,128)}, f32[512,512]{1,0:T(8,128)S(1)}, s32[]{:T(128)}, s32[512]{0:T(512)}, /*index=5*/s32[512]{0:T(512)}, bf16...) while((s32[]{:T(128)}, f32[128,512]{1,0:T(8,128)}, ...), condition=%wide.region_7.10_spmd, body=%wide.region_6.9_spmd.sunk | while | flops 168314624 | bytes 2367799 | solution.py:86
  183.9 2.0 convolution_add_fusion.14
  190.1 2.0 convolution_add_fusion.14
  196.4 2.0 convolution_add_fusion.14
  200.3 22.2 %while.48 = (s32[]{:T(128)}, f32[512,512]{1,0:T(8,128)S(1)}, f32[384,512]{1,0:T(8,128)S(1)}, s32[]{:T(128)}, s32[512]{0:T(512)}, /*index=5*/bf16[384,512]{1,0:T(...) while((s32[]{:T(128)}, f32[512,512]{1,0:T(8,128)S(1)}, ...), condition=%wide.region_9.12_spmd, body=%wide.region_8.11_spmd.sunk | while | flops 438357888 | bytes 8272603 | solution.py:111
  204.1 1.5 convolution_add_fusion.15
  218.4 1.5 convolution_add_fusion.15
  223.9 6.1 %collective-permute-start.5 = (f32[128,512]{1,0:T(8,128)S(1)}, f32[128,512]{1,0:T(8,128)S(1)}, u32[]{:S(2)}, u32[]{:S(2)}) collective-permute-start(f32[128,512]{1,0:T(8,128)S(1)} %get-tuple-element.310), channel_id=1, source_target_pairs={{0,1},{1,2},{2,3},{3,4},{4,5},{5,6},{6,7},{7,8},{8,9},{9,10},{10,1... | collective-permute-start | bytes 786440 | tf_op jit(solution)/shard_map/ppermute | solution.py:26
  231.1 1.6 fusion.48
  232.8 53.1 %all-reduce.11.cloned.1.call-done = f32[128,512]{1,0:T(8,128)} async-done(((f32[128,512]{1,0:T(8,128)}), f32[128,512]{1,0:T(8,128)}) %all-reduce.11.cloned.1.call-update) | async-done | bytes 262160 | tf_op jit(solution)/shard_map/psum | solution.py:205
  285.9 2.5 fusion.42
  288.5 79.6 %all-reduce.13.cloned.1.call-done = f32[512,512]{1,0:T(8,128)} async-done(((f32[512,512]{1,0:T(8,128)}), f32[512,512]{1,0:T(8,128)}) %all-reduce.13.cloned.1.call-update) | async-done | bytes 1048592 | tf_op jit(solution)/shard_map/psum | solution.py:207
  368.1 1.9 multiply_convert_fusion.5
  371.4 1.6 convolution_add_fusion.7
  375.1 18.6 %while.49 = (s32[]{:T(128)}, f32[512,512]{1,0:T(8,128)S(1)}, s32[]{:T(128)}, s32[1024]{0:T(1024)}, bf16[384,512]{1,0:T(8,128)(2,1)S(1)}, /*index=5*/s32[1024]{0:...) while((s32[]{:T(128)}, f32[512,512]{1,0:T(8,128)S(1)}, ...), condition=%wide.region_13.16_spmd, body=%wide.region_12.15_spmd.sunk | while | flops 68161032 | bytes 3551915 | solution.py:111
  393.7 2.8 convolution_multiply_fusion
  398.2 2.7 fusion.44
  400.9 152.5 %all-reduce.15.cloned.1.call-done = (f32[512,512]{1,0:T(8,128)}, f32[512,512]{1,0:T(8,128)}, f32[512,512]{1,0:T(8,128)}) async-done(((f32[512,512]{1,0:T(8,128)}, f32[512,512]{1,0:T(8,128)}, f32[512,512]{1,0:T(8,128)}), (f32[512,512]{1,0:T(8,128)}, f32[512,512]{1,0:T(8,128)}, f32[512,512]{1,0:T(8,128)})) %all-reduce.15.cloned.1.call-update) | async-done | bytes 3145744 | tf_op jit(solution)/shard_map/psum | solution.py:230
  553.4 2.4 copy.68
  (195 shorter events, 73.4 us)
Async XLA Ops:
  7.2 161.6 %copy-start = (bf16[512,512]{1,0:T(8,128)(2,1)S(1)}, bf16[512,512]{1,0:T(8,128)(2,1)}, u32[]{:S(2)}) copy-start(bf16[512,512]{1,0:T(8,128)(2,1)} %param.40) | copy-start | bytes 1572868
  7.2 9.8 %copy-start.5 = (bf16[512,512]{1,0:T(8,128)(2,1)S(1)}, bf16[512,512]{1,0:T(8,128)(2,1)}, u32[]{:S(2)}) copy-start(bf16[512,512]{1,0:T(8,128)(2,1)} %param.37) | copy-start | bytes 1572868
  7.2 79.2 %all-reduce.7.cloned.1.call-start = ((), (), s32[]{:S(2)}) async-start(), calls=%async_computation | async-start | bytes 524288 | tf_op jit(solution)/shard_map/psum | solution.py:159
  7.2 6.5 %collective-permute-start = (bf16[128,512]{1,0:T(8,128)(2,1)}, bf16[128,512]{1,0:T(8,128)(2,1)S(1)}, u32[]{:S(2)}, u32[]{:S(2)}) collective-permute-start(bf16[128,512]{1,0:T(8,128)(2,1)} %param.27), channel_id=1, source_target_pairs={{0,1},{1,2},{2,3},{3,4},{4,5},{5,6},{6,7},{7,8},{8,9},{9,10},{10,1... | collective-permute-start | bytes 393224 | tf_op jit(solution)/shard_map/ppermute | solution.py:17
  9.8 5.6 collective-permute-start.1
  12.5 78.5 %copy-start.21 = (s32[128]{0:T(128)}, s32[128]{0:T(128)S(1)}, u32[]{:S(2)}) copy-start(s32[128]{0:T(128)S(1)} %get-tuple-element.300) | copy-start | bytes 1540
  17.0 16.4 %copy-start.14 = (bf16[128,512]{1,0:T(8,128)(2,1)S(1)}, bf16[128,512]{1,0:T(8,128)(2,1)}, u32[]{:S(2)}) copy-start(bf16[128,512]{1,0:T(8,128)(2,1)} %param.28) | copy-start | bytes 393220
  17.0 69.3 %copy-start.26 = (bf16[512,512]{1,0:T(8,128)(2,1)S(1)}, bf16[512,512]{1,0:T(8,128)(2,1)}, u32[]{:S(2)}) copy-start(bf16[512,512]{1,0:T(8,128)(2,1)} %param.39) | copy-start | bytes 1572868
  33.3 56.3 %copy-start.18 = (s32[1024]{0:T(1024)}, s32[1024]{0:T(1024)S(1)}, u32[]{:S(2)}) copy-start(s32[1024]{0:T(1024)S(1)} %get-tuple-element.780) | copy-start | bytes 12292
  33.4 56.3 %copy-start.19 = (s32[1024]{0:T(1024)}, s32[1024]{0:T(1024)S(1)}, u32[]{:S(2)}) copy-start(s32[1024]{0:T(1024)S(1)} %get-tuple-element.781) | copy-start | bytes 12292
  33.4 55.0 %copy-start.1 = (s32[128]{0:T(128)S(1)}, s32[128]{0:T(128)}, u32[]{:S(2)}) copy-start(s32[128]{0:T(128)} %param.36) | copy-start | bytes 1540
  34.3 134.4 %all-reduce.9.cloned.1.call-start = ((), (), s32[]{:S(2)}) async-start(), calls=%async_computation.1 | async-start | bytes 2097152 | tf_op jit(solution)/shard_map/psum | solution.py:165
  89.7 196.2 %all-reduce.11.cloned.1.call-start = ((), (), s32[]{:S(2)}) async-start(), calls=%async_computation.2 | async-start | bytes 524288 | tf_op jit(solution)/shard_map/psum | solution.py:205
  91.0 81.3 %copy-start.23 = (pred[128]{0:T(512)(128)(4,1)}, pred[128]{0:T(512)(128)(4,1)S(1)}, u32[]{:S(2)}) copy-start(pred[128]{0:T(512)(128)(4,1)S(1)} %get-tuple-element.298) | copy-start | bytes 388
  91.9 83.6 %copy-start.20 = (s32[512]{0:T(512)S(1)}, s32[512]{0:T(512)}, u32[]{:S(2)}) copy-start(s32[512]{0:T(512)} %param.34) | copy-start | bytes 6148
  91.9 83.6 %copy-start.25 = (s32[512]{0:T(512)S(1)}, s32[512]{0:T(512)}, u32[]{:S(2)}) copy-start(s32[512]{0:T(512)} %param.33) | copy-start | bytes 6148
  171.4 8.2 %copy-start.6 = (bf16[512,512]{1,0:T(8,128)(2,1)S(1)}, bf16[512,512]{1,0:T(8,128)(2,1)}, u32[]{:S(2)}) copy-start(bf16[512,512]{1,0:T(8,128)(2,1)} %param.38) | copy-start | bytes 1572868
  172.4 4.2 collective-permute-start.2
  174.1 4.6 collective-permute-start.3
  179.6 20.7 %copy-start.2 = (bf16[128,512]{1,0:T(8,128)(2,1)S(1)}, bf16[128,512]{1,0:T(8,128)(2,1)}, u32[]{:S(2)}) copy-start(bf16[128,512]{1,0:T(8,128)(2,1)} %param.41) | copy-start | bytes 393220
  222.5 65.9 %copy-start.3 = (f32[512,512]{1,0:T(8,128)}, f32[512,512]{1,0:T(8,128)S(1)}, u32[]{:S(2)}) copy-start(f32[512,512]{1,0:T(8,128)S(1)} %get-tuple-element.208) | copy-start | bytes 3145732
  222.6 7.4 %collective-permute-start.4 = (f32[128,512]{1,0:T(8,128)S(1)}, f32[128,512]{1,0:T(8,128)S(1)}, u32[]{:S(2)}, u32[]{:S(2)}) collective-permute-start(f32[128,512]{1,0:T(8,128)S(1)} %get-tuple-element.309), channel_id=1, source_target_pairs={{1,0},{2,1},{3,2},{4,3},{5,4},{6,5},{7,6},{8,7},{9,8},{10,9},{11,1... | collective-permute-start | bytes 786440 | tf_op jit(solution)/shard_map/ppermute | solution.py:26
  223.9 7.2 %collective-permute-start.5 = (f32[128,512]{1,0:T(8,128)S(1)}, f32[128,512]{1,0:T(8,128)S(1)}, u32[]{:S(2)}, u32[]{:S(2)}) collective-permute-start(f32[128,512]{1,0:T(8,128)S(1)} %get-tuple-element.310), channel_id=1, source_target_pairs={{0,1},{1,2},{2,3},{3,4},{4,5},{5,6},{6,7},{7,8},{8,9},{9,10},{10,1... | collective-permute-start | bytes 786440 | tf_op jit(solution)/shard_map/ppermute | solution.py:26
  231.1 138.9 %copy-start.11 = (f32[128,512]{1,0:T(8,128)}, f32[128,512]{1,0:T(8,128)S(1)}, u32[]{:S(2)}) copy-start(f32[128,512]{1,0:T(8,128)S(1)} %collective-permute-done.5) | copy-start | bytes 786436
  232.7 135.3 %all-reduce.13.cloned.1.call-start = ((), (), s32[]{:S(2)}) async-start(), calls=%async_computation.3 | async-start | bytes 2097152 | tf_op jit(solution)/shard_map/psum | solution.py:207
  288.4 264.9 %all-reduce.15.cloned.1.call-start = ((), (), s32[]{:S(2)}) async-start(), calls=%async_computation.4 | async-start | bytes 6291456 | tf_op jit(solution)/shard_map/psum | solution.py:230
  371.3 2.5 copy-start.16
  371.4 2.5 copy-start.24
  375.1 18.6 %copy-start.15 = (f32[128,512]{1,0:T(8,128)S(1)}, f32[128,512]{1,0:T(8,128)}, u32[]{:S(2)}) copy-start(f32[128,512]{1,0:T(8,128)} %all-reduce.11.cloned.1.call-done) | copy-start | bytes 786436
  375.1 18.6 %copy-start.17 = (bf16[128,512]{1,0:T(8,128)(2,1)S(1)}, bf16[128,512]{1,0:T(8,128)(2,1)}, u32[]{:S(2)}) copy-start(bf16[128,512]{1,0:T(8,128)(2,1)} %copy-done.16) | copy-start | bytes 393220
  393.7 2.8 copy-start.4
  553.4 3.4 copy-start.9
  (8 other events, 12.1 us)
Sparse Core Ops, SparseCore 0:
  34.4 51.8 all-reduce.6
  90.4 78.2 all-reduce.8
  232.9 52.9 all-reduce.10
  289.8 78.2 all-reduce.12
  396.7 156.6 all-reduce.14
where the time goes:
time: 566 us; the launch traced here: 564 us
  waiting for transfers between devices  418 us (74%)
  matrix products  53.6 us (9%)
  local copies, waits for them, and re-layouts  34.9 us (6%)
  other arithmetic  17.7 us (3%)
  starting transfers between devices  14.4 us (3%)
  between operations  14.3 us (3%)
  loops' own time  11.6 us (2%)
    psum x1, waiting for transfers between devices, shards(): lax.psum((encode_local, decode_local, sub_share * middle_local), ('tile',...  152 us
    psum x1, waiting for transfers between devices, shards(): summit_grad_whole = lax.psum(summit_grad_part, 'tile')  79.6 us
    psum x1, waiting for transfers between devices, shards(): summit_whole = lax.psum(summit_part, 'tile')  76.8 us
    psum x1, waiting for transfers between devices, shards(): level_grad = lax.psum(level_part, 'sub')  53.1 us
    psum x1, waiting for transfers between devices, shards(): middle_sum = lax.psum(middle_part, 'sub')  52 us
    dot_general x9, matrix products, outer_sum(): lax.dot_general(left, right, (((0,), (0,)), ((), ())), preferred_element_...  16 us
    dot_general x12, matrix products, exact_sum(): jnp.dot(members, values, precision=lax.Precision.HIGHEST, preferred_eleme...  13.6 us
    gather x14, local copies, waits for them, and re-layouts, block_step(): fetched = jnp.take(sources, picked, axis=0)  11.9 us
  transfers between devices with their start and end apart: 11, of which 8 were waited for; matrix products, arithmetic and copies ran while one was open for 2% of the time, Pallas kernels for 0%

commit v1 on v0

--- a/solution.py
+++ b/solution.py
@@ -228,7 +228,7 @@
     )
     sub_share = 1.0 / subs
     encode_grad, decode_grad, middle_grad = lax.psum(
-        (encode_local, decode_local, sub_share * middle_local), ("tile", "sub")
+        lax.psum((encode_local, decode_local, sub_share * middle_local), "sub"), "tile"
     )
     return (grid_update, encode_grad, decode_grad, middle_grad, summit_local)
 

time: 566 us -> 629 us (1.11)
  waiting for transfers between devices: 418 us -> 482 us
    psum x1 -> x2, waiting for transfers between devices: 152 us -> 217 us  [the longest x1 131 us: shards(): lax.psum(lax.psum((encode_local, decode_local, sub_share * middle_local),...]
  transfers between devices with their start and end apart: 11 -> 12, of which waited for: 8 -> 9; matrix products, arithmetic and copies ran while one was open for 2% -> 1% of each run, Pallas kernels for 0% -> 0%
where the time goes in v1:
time: 629 us; the launch traced here: 627 us
  waiting for transfers between devices  482 us (77%)
  matrix products  52.3 us (8%)
  local copies, waits for them, and re-layouts  33.9 us (5%)
  other arithmetic  17.6 us (3%)
  between operations  14.7 us (2%)
  starting transfers between devices  14.4 us (2%)
  loops' own time  12 us (2%)
    psum x1, waiting for transfers between devices, shards(): lax.psum(lax.psum((encode_local, decode_local, sub_share * middle_local),...  131 us
    psum x1, waiting for transfers between devices, shards(): lax.psum((encode_local, decode_local, sub_share * middle_local), 'sub')  86.4 us
    psum x1, waiting for transfers between devices, shards(): summit_grad_whole = lax.psum(summit_grad_part, 'tile')  79.6 us
    psum x1, waiting for transfers between devices, shards(): summit_whole = lax.psum(summit_part, 'tile')  76.8 us
    psum x1, waiting for transfers between devices, shards(): level_grad = lax.psum(level_part, 'sub')  53 us
    psum x1, waiting for transfers between devices, shards(): middle_sum = lax.psum(middle_part, 'sub')  52.3 us
    dot_general x9, matrix products, outer_sum(): lax.dot_general(left, right, (((0,), (0,)), ((), ())), preferred_element_...  14.8 us
    dot_general x12, matrix products, exact_sum(): jnp.dot(members, values, precision=lax.Precision.HIGHEST, preferred_eleme...  13.6 us
  transfers between devices with their start and end apart: 12, of which 9 were waited for; matrix products, arithmetic and copies ran while one was open for 1% of the time, Pallas kernels for 0%

profile of v1, /device:TPU:0, one launch (start us, length us, event | category | flops | bytes accessed | tf_op | source)
XLA Modules:
  0.0 627.3 jit_solution(15287925458555477253)
XLA Ops:
  7.2 2.5 collective-permute-start
  15.4 1.6 broadcast_in_dim.93
  17.0 16.6 %while.46 = (s32[]{:T(128)}, f32[128,512]{1,0:T(8,128)S(1)}, f32[1024,512]{1,0:T(8,128)}, s32[]{:T(128)}, s32[1024]{0:T(1024)S(1)}, /*index=5*/s32[1024]{0:T(102...) while((s32[]{:T(128)}, f32[128,512]{1,0:T(8,128)S(1)}, ...), condition=%wide.region_3.5_spmd, body=%wide.region_2.0_spmd.sunk | while | flops 168314624 | bytes 2367415 | solution.py:86
  18.7 1.9 constant_dynamic-update-slice_fusion.7
  22.6 1.9 constant_dynamic-update-slice_fusion.7
  26.6 1.9 constant_dynamic-update-slice_fusion.7
  30.6 1.9 constant_dynamic-update-slice_fusion.7
  34.6 52.3 %all-reduce.9.cloned.1.call-done = f32[128,512]{1,0:T(8,128)} async-done(((f32[128,512]{1,0:T(8,128)}), f32[128,512]{1,0:T(8,128)}) %all-reduce.9.cloned.1.call-update) | async-done | bytes 262160 | tf_op jit(solution)/shard_map/psum | solution.py:159
  86.9 2.0 add_convert_fusion.2
  92.4 76.8 %all-reduce.11.cloned.1.call-done = f32[512,512]{1,0:T(8,128)} async-done(((f32[512,512]{1,0:T(8,128)}), f32[512,512]{1,0:T(8,128)}) %all-reduce.11.cloned.1.call-update) | async-done | bytes 1048592 | tf_op jit(solution)/shard_map/psum | solution.py:165
  169.3 2.7 multiply_convert_fusion.6
  173.0 1.7 collective-permute-start.2
  177.2 2.0 collective-permute-done.3
  180.1 19.3 %while.47 = (s32[]{:T(128)}, f32[128,512]{1,0:T(8,128)}, f32[512,512]{1,0:T(8,128)S(1)}, s32[]{:T(128)}, s32[512]{0:T(512)}, /*index=5*/s32[512]{0:T(512)}, bf16...) while((s32[]{:T(128)}, f32[128,512]{1,0:T(8,128)}, ...), condition=%wide.region_7.10_spmd, body=%wide.region_6.9_spmd.sunk | while | flops 168314624 | bytes 2367799 | solution.py:86
  184.4 2.0 convolution_add_fusion.14
  190.6 2.0 convolution_add_fusion.14
  196.8 2.0 convolution_add_fusion.14
  200.6 21.9 %while.48 = (s32[]{:T(128)}, f32[512,512]{1,0:T(8,128)S(1)}, f32[384,512]{1,0:T(8,128)S(1)}, s32[]{:T(128)}, s32[512]{0:T(512)}, /*index=5*/bf16[384,512]{1,0:T(...) while((s32[]{:T(128)}, f32[512,512]{1,0:T(8,128)S(1)}, ...), condition=%wide.region_9.12_spmd, body=%wide.region_8.11_spmd.sunk | while | flops 438357888 | bytes 8272603 | solution.py:111
  211.4 1.5 convolution_add_fusion.15
  218.5 1.5 convolution_add_fusion.15
  223.9 6.1 collective-permute-start.5
  231.2 1.6 fusion.48
  232.9 53.0 %all-reduce.13.cloned.1.call-done = f32[128,512]{1,0:T(8,128)} async-done(((f32[128,512]{1,0:T(8,128)}), f32[128,512]{1,0:T(8,128)}) %all-reduce.13.cloned.1.call-update) | async-done | bytes 262160 | tf_op jit(solution)/shard_map/psum | solution.py:205
  285.8 2.5 fusion.42
  288.5 79.6 %all-reduce.15.cloned.1.call-done = f32[512,512]{1,0:T(8,128)} async-done(((f32[512,512]{1,0:T(8,128)}), f32[512,512]{1,0:T(8,128)}) %all-reduce.15.cloned.1.call-update) | async-done | bytes 1048592 | tf_op jit(solution)/shard_map/psum | solution.py:207
  368.0 1.9 multiply_convert_fusion.5
  371.3 1.6 convolution_add_fusion.7
  375.1 18.9 %while.49 = (s32[]{:T(128)}, f32[512,512]{1,0:T(8,128)S(1)}, s32[]{:T(128)}, s32[1024]{0:T(1024)}, bf16[384,512]{1,0:T(8,128)(2,1)S(1)}, /*index=5*/s32[1024]{0:...) while((s32[]{:T(128)}, f32[512,512]{1,0:T(8,128)S(1)}, ...), condition=%wide.region_13.16_spmd, body=%wide.region_12.15_spmd.sunk | while | flops 68161032 | bytes 3551915 | solution.py:111
  394.0 2.8 convolution_multiply_fusion
  396.9 86.4 %all-reduce.19.cloned.1.call-done = (f32[512,512]{1,0:T(8,128)}, f32[512,512]{1,0:T(8,128)}, f32[512,512]{1,0:T(8,128)}) async-done(((f32[512,512]{1,0:T(8,128)}, f32[512,512]{1,0:T(8,128)}, f32[512,512]{1,0:T(8,128)}), (f32[512,512]{1,0:T(8,128)}, f32[512,512]{1,0:T(8,128)}, f32[512,512]{1,0:T(8,128)})) %all-reduce.19.cloned.1.call-update) | async-done | bytes 3145744 | tf_op jit(solution)/shard_map/psum | solution.py:231
  485.5 130.6 %all-reduce.17.cloned.1.call-done = (f32[512,512]{1,0:T(8,128)}, f32[512,512]{1,0:T(8,128)}, f32[512,512]{1,0:T(8,128)}) async-done(((f32[512,512]{1,0:T(8,128)}, f32[512,512]{1,0:T(8,128)}, f32[512,512]{1,0:T(8,128)}), (f32[512,512]{1,0:T(8,128)}, f32[512,512]{1,0:T(8,128)}, f32[512,512]{1,0:T(8,128)})) %all-reduce.17.cloned.1.call-update) | async-done | bytes 3145744 | tf_op jit(solution)/shard_map/psum | solution.py:230
  616.1 2.4 copy.71
  (200 shorter events, 73.9 us)
Async XLA Ops:
  7.2 162.1 %copy-start = (bf16[512,512]{1,0:T(8,128)(2,1)S(1)}, bf16[512,512]{1,0:T(8,128)(2,1)}, u32[]{:S(2)}) copy-start(bf16[512,512]{1,0:T(8,128)(2,1)} %param.40) | copy-start | bytes 1572868
  7.2 9.8 %copy-start.5 = (bf16[512,512]{1,0:T(8,128)(2,1)S(1)}, bf16[512,512]{1,0:T(8,128)(2,1)}, u32[]{:S(2)}) copy-start(bf16[512,512]{1,0:T(8,128)(2,1)} %param.37) | copy-start | bytes 1572868
  7.2 79.7 %all-reduce.9.cloned.1.call-start = ((), (), s32[]{:S(2)}) async-start(), calls=%async_computation | async-start | bytes 524288 | tf_op jit(solution)/shard_map/psum | solution.py:159
  7.2 6.6 %collective-permute-start = (bf16[128,512]{1,0:T(8,128)(2,1)}, bf16[128,512]{1,0:T(8,128)(2,1)S(1)}, u32[]{:S(2)}, u32[]{:S(2)}) collective-permute-start(bf16[128,512]{1,0:T(8,128)(2,1)} %param.27), channel_id=1, source_target_pairs={{0,1},{1,2},{2,3},{3,4},{4,5},{5,6},{6,7},{7,8},{8,9},{9,10},{10,1... | collective-permute-start | bytes 393224 | tf_op jit(solution)/shard_map/ppermute | solution.py:17
  9.8 5.6 collective-permute-start.1
  12.5 79.1 %copy-start.22 = (s32[128]{0:T(128)}, s32[128]{0:T(128)S(1)}, u32[]{:S(2)}) copy-start(s32[128]{0:T(128)S(1)} %get-tuple-element.303) | copy-start | bytes 1540
  17.0 16.6 %copy-start.15 = (bf16[128,512]{1,0:T(8,128)(2,1)S(1)}, bf16[128,512]{1,0:T(8,128)(2,1)}, u32[]{:S(2)}) copy-start(bf16[128,512]{1,0:T(8,128)(2,1)} %param.28) | copy-start | bytes 393220
  17.0 69.9 %copy-start.27 = (bf16[512,512]{1,0:T(8,128)(2,1)S(1)}, bf16[512,512]{1,0:T(8,128)(2,1)}, u32[]{:S(2)}) copy-start(bf16[512,512]{1,0:T(8,128)(2,1)} %param.39) | copy-start | bytes 1572868
  33.6 56.6 %copy-start.19 = (s32[1024]{0:T(1024)}, s32[1024]{0:T(1024)S(1)}, u32[]{:S(2)}) copy-start(s32[1024]{0:T(1024)S(1)} %get-tuple-element.797) | copy-start | bytes 12292
  33.6 56.6 %copy-start.20 = (s32[1024]{0:T(1024)}, s32[1024]{0:T(1024)S(1)}, u32[]{:S(2)}) copy-start(s32[1024]{0:T(1024)S(1)} %get-tuple-element.798) | copy-start | bytes 12292
  33.6 55.3 %copy-start.1 = (s32[128]{0:T(128)S(1)}, s32[128]{0:T(128)}, u32[]{:S(2)}) copy-start(s32[128]{0:T(128)} %param.36) | copy-start | bytes 1540
  34.6 134.7 %all-reduce.11.cloned.1.call-start = ((), (), s32[]{:S(2)}) async-start(), calls=%async_computation.1 | async-start | bytes 2097152 | tf_op jit(solution)/shard_map/psum | solution.py:165
  90.2 195.6 %all-reduce.13.cloned.1.call-start = ((), (), s32[]{:S(2)}) async-start(), calls=%async_computation.2 | async-start | bytes 524288 | tf_op jit(solution)/shard_map/psum | solution.py:205
  90.3 79.0 %copy-start.23 = (s32[1024]{0:T(1024)}, s32[1024]{0:T(1024)S(1)}, u32[]{:S(2)}) copy-start(s32[1024]{0:T(1024)S(1)} %pad_clamp_fusion.8) | copy-start | bytes 12292
  91.5 81.3 %copy-start.24 = (pred[128]{0:T(512)(128)(4,1)}, pred[128]{0:T(512)(128)(4,1)S(1)}, u32[]{:S(2)}) copy-start(pred[128]{0:T(512)(128)(4,1)S(1)} %get-tuple-element.301) | copy-start | bytes 388
  92.4 83.5 %copy-start.21 = (s32[512]{0:T(512)S(1)}, s32[512]{0:T(512)}, u32[]{:S(2)}) copy-start(s32[512]{0:T(512)} %param.34) | copy-start | bytes 6148
  92.4 83.5 %copy-start.26 = (s32[512]{0:T(512)S(1)}, s32[512]{0:T(512)}, u32[]{:S(2)}) copy-start(s32[512]{0:T(512)} %param.33) | copy-start | bytes 6148
  173.0 4.3 collective-permute-start.2
  174.6 4.6 collective-permute-start.3
  180.1 20.5 %copy-start.2 = (bf16[128,512]{1,0:T(8,128)(2,1)S(1)}, bf16[128,512]{1,0:T(8,128)(2,1)}, u32[]{:S(2)}) copy-start(bf16[128,512]{1,0:T(8,128)(2,1)} %param.41) | copy-start | bytes 393220
  222.6 65.8 %copy-start.3 = (f32[512,512]{1,0:T(8,128)}, f32[512,512]{1,0:T(8,128)S(1)}, u32[]{:S(2)}) copy-start(f32[512,512]{1,0:T(8,128)S(1)} %get-tuple-element.208) | copy-start | bytes 3145732
  222.6 7.4 %collective-permute-start.4 = (f32[128,512]{1,0:T(8,128)S(1)}, f32[128,512]{1,0:T(8,128)S(1)}, u32[]{:S(2)}, u32[]{:S(2)}) collective-permute-start(f32[128,512]{1,0:T(8,128)S(1)} %get-tuple-element.312), channel_id=1, source_target_pairs={{1,0},{2,1},{3,2},{4,3},{5,4},{6,5},{7,6},{8,7},{9,8},{10,9},{11,1... | collective-permute-start | bytes 786440 | tf_op jit(solution)/shard_map/ppermute | solution.py:26
  223.9 7.2 %collective-permute-start.5 = (f32[128,512]{1,0:T(8,128)S(1)}, f32[128,512]{1,0:T(8,128)S(1)}, u32[]{:S(2)}, u32[]{:S(2)}) collective-permute-start(f32[128,512]{1,0:T(8,128)S(1)} %get-tuple-element.313), channel_id=1, source_target_pairs={{0,1},{1,2},{2,3},{3,4},{4,5},{5,6},{6,7},{7,8},{8,9},{9,10},{10,1... | collective-permute-start | bytes 786440 | tf_op jit(solution)/shard_map/ppermute | solution.py:26
  231.2 138.8 %copy-start.12 = (f32[128,512]{1,0:T(8,128)}, f32[128,512]{1,0:T(8,128)S(1)}, u32[]{:S(2)}) copy-start(f32[128,512]{1,0:T(8,128)S(1)} %collective-permute-done.5) | copy-start | bytes 786436
  232.8 135.2 %all-reduce.15.cloned.1.call-start = ((), (), s32[]{:S(2)}) async-start(), calls=%async_computation.3 | async-start | bytes 2097152 | tf_op jit(solution)/shard_map/psum | solution.py:207
  288.4 194.9 %all-reduce.19.cloned.1.call-start = ((), (), s32[]{:S(2)}) async-start(), calls=%async_computation.5 | async-start | bytes 6291456 | tf_op jit(solution)/shard_map/psum | solution.py:231
  375.0 18.9 %copy-start.16 = (f32[128,512]{1,0:T(8,128)S(1)}, f32[128,512]{1,0:T(8,128)}, u32[]{:S(2)}) copy-start(f32[128,512]{1,0:T(8,128)} %all-reduce.13.cloned.1.call-done) | copy-start | bytes 786436
  375.1 18.9 %copy-start.18 = (bf16[128,512]{1,0:T(8,128)(2,1)S(1)}, bf16[128,512]{1,0:T(8,128)(2,1)}, u32[]{:S(2)}) copy-start(bf16[128,512]{1,0:T(8,128)(2,1)} %copy-done.17) | copy-start | bytes 393220
  396.9 86.5 %copy-start.13 = (f32[128,512]{1,0:T(8,128)S(1)}, f32[128,512]{1,0:T(8,128)}, u32[]{:S(2)}) copy-start(f32[128,512]{1,0:T(8,128)} %get-tuple-element.203) | copy-start | bytes 786436
  396.9 86.5 %copy-start.14 = (bf16[128,512]{1,0:T(8,128)(2,1)S(1)}, bf16[128,512]{1,0:T(8,128)(2,1)}, u32[]{:S(2)}) copy-start(bf16[128,512]{1,0:T(8,128)(2,1)} %param.27) | copy-start | bytes 393220
  396.9 87.2 %copy-start.9 = (f32[512,512]{1,0:T(8,128)S(1)}, f32[512,512]{1,0:T(8,128)}, u32[]{:S(2)}) copy-start(f32[512,512]{1,0:T(8,128)} %all-reduce.11.cloned.1.call-done) | copy-start | bytes 3145732
  396.9 219.2 %all-reduce.17.cloned.1.call-start = ((), (), s32[]{:S(2)}) async-start(), calls=%async_computation.4 | async-start | bytes 6291456 | tf_op jit(solution)/shard_map/psum | solution.py:230
  (10 other events, 27.5 us)
Sparse Core Ops, SparseCore 0:
  34.7 52.1 all-reduce.8
  91.0 78.1 all-reduce.10
  232.9 52.8 all-reduce.12
  289.8 78.2 all-reduce.14
  397.0 86.2 all-reduce.18
  487.1 128.9 all-reduce.16
